TPU v7x, 256 devices: a whole 4x4x8 slice. The times are simulated.
256 devices in a mesh: cells: 256 (over z, x, y, core).
Axes of the slice: x: 4, y: 4, z: 8, core: 2. Of those that a mesh axis runs over, the one named last changes fastest.
Arguments:
- field: float32 [9, 55, 262144], P(None, None, 'cells'), may hold values from -6 to 6
- cell_area: float32 [262144], P('cells'), may hold values from 0.5 to 2
- dv_edge: float32 [827392], P('cells'), may hold values from 0.6 to 1.6
- dc_edge: float32 [827392], P('cells'), may hold values from 0.6 to 1.6
- cells_on_edge: int32 [2, 827392], P(None, 'cells'), may hold values from 0 to 1407, as said below
- edges_on_cell: int32 [6, 262144], P(None, 'cells'), may hold values from 0 to 3231, as said below
- send_cells: int32 [6, 16384], P(None, 'cells'), may hold values from 0 to 1023
- level_coef: float32 [55], replicated, may hold values from 0.005 to 0.02
Outputs:
- tendency: float32 [9, 55, 262144], P(None, None, 'cells')
Inputs may be any that keep to these rules, and one draw needn't show every extreme that they name: `cells_on_edge`: the blocks tile one periodic hexagonal mesh, each a parallelogram of 64 by 16 cells; block b borders b + 1 and b - 1 along the first direction, b + 16 and b - 16 along the second, and b + 15 and b - 15 at one cell each, all modulo 256. Every edge with a cell in a block is listed once in that block, with the same dv_edge and dc_edge wherever it is listed, plus one extra entry that no cell names. Cells and edges are numbered in random order in each block. `edges_on_cell`: each cell names six distinct edges of its block.
All inputs are finite; a program needn't handle non-finite values.
Results may differ from a plain program's by a relative error of at most 0.00005.
Values sent between devices are 32-bit elements; how exact they have to be, the bound alone decides.
A program may use at most 128 MiB of HBM per device.

v0:
```python
import jax
import jax.numpy as jnp
from jax import lax
from jax.sharding import PartitionSpec as P

CELLS_Y = 16
BLOCK_ROW = 16


def from_behind(x, axis, by):
    devices = lax.axis_size(axis)
    return lax.ppermute(x, axis, [(i, (i + by) % devices) for i in range(devices)])


def widen(piece, length):
    return jnp.pad(piece, ((0, 0), (0, length - piece.shape[1])))


def shards(
    field, cell_area, dv_edge, dc_edge, cells_on_edge, edges_on_cell, send_cells, level_coef
):
    length = send_cells.shape[1]
    side = CELLS_Y
    fields_n = field.shape[0]
    levels_n = field.shape[1]
    cell_count = field.shape[2]
    edge_count = dv_edge.shape[0]
    ext_count = cell_count + 6 * length
    rows_n = fields_n * levels_n
    highest = lax.Precision.HIGHEST
    weight = dv_edge / dc_edge
    first_end = jnp.take(cells_on_edge[0], edges_on_cell)
    own_index = lax.broadcasted_iota(jnp.int32, edges_on_cell.shape, 1)
    orient = jnp.where(first_end == own_index, 1.0, -1.0).astype(jnp.float32)
    cell_ids = lax.broadcasted_iota(jnp.int32, (cell_count, 6 * length), 0)
    selector = (cell_ids == send_cells.reshape(1, 6 * length)).astype(jnp.float32)
    ext_ids = lax.broadcasted_iota(jnp.int32, (ext_count, edge_count), 0)
    differ = (
        (ext_ids == cells_on_edge[1][None, :]).astype(jnp.float32)
        - (ext_ids == cells_on_edge[0][None, :]).astype(jnp.float32)
    ) * weight[None, :]
    edge_ids = lax.broadcasted_iota(jnp.int32, (edge_count, cell_count), 0)
    collect = jnp.zeros((edge_count, cell_count), jnp.float32)
    for slot_j in range(6):
        collect = collect + jnp.where(
            edge_ids == edges_on_cell[slot_j][None, :], orient[slot_j][None, :], 0.0
        )
    collect = collect / cell_area[None, :]
    operator = jnp.dot(differ, collect, precision=highest, preferred_element_type=jnp.float32)

    def extend(values):
        picked = jnp.dot(
            values, selector, precision=highest, preferred_element_type=jnp.float32
        ).reshape(rows_n, 6, length)
        toward_right = picked[:, 0, :side]
        toward_left = picked[:, 1, :side]
        toward_upper = picked[:, 2, :]
        toward_lower = picked[:, 3, :]
        corner_upper = picked[:, 4, :1]
        corner_lower = picked[:, 5, :1]
        carried_back = from_behind(
            jnp.concatenate([toward_left, corner_upper], axis=1), "cells", -1
        )
        carried_fore = from_behind(
            jnp.concatenate([toward_right, corner_lower], axis=1), "cells", 1
        )
        from_right = carried_back[:, :side]
        from_left = carried_fore[:, :side]
        carried_up = from_behind(
            jnp.concatenate([toward_upper, carried_back[:, side:]], axis=1), "cells", BLOCK_ROW
        )
        carried_down = from_behind(
            jnp.concatenate([toward_lower, carried_fore[:, side:]], axis=1), "cells", -BLOCK_ROW
        )
        from_below = carried_up[:, :length]
        corner_below = carried_up[:, length:]
        from_above = carried_down[:, :length]
        corner_above = carried_down[:, length:]
        return jnp.concatenate(
            [
                values,
                widen(from_left, length),
                widen(from_right, length),
                from_below,
                from_above,
                widen(corner_below, length),
                widen(corner_above, length),
            ],
            axis=1,
        )

    def laplacian(values):
        extended = extend(values)
        return jnp.dot(extended, operator, precision=highest, preferred_element_type=jnp.float32)

    flat = field.reshape(rows_n, cell_count)
    first_pass = laplacian(flat)
    second_pass = laplacian(first_pass).reshape(fields_n, levels_n, cell_count)
    return -level_coef[None, :, None] * second_pass


def solution(mesh):
    return jax.shard_map(
        shards,
        mesh=mesh,
        in_specs=(
            P(None, None, "cells"),
            P("cells"),
            P("cells"),
            P("cells"),
            P(None, "cells"),
            P(None, "cells"),
            P(None, "cells"),
            P(),
        ),
        out_specs=P(None, None, "cells"),
        check_vma=False,
    )
```

profile of v0, /device:TPU:27, one launch (start us, length us, event | category | flops | bytes accessed | tf_op | source)
XLA Modules:
  0.0 230.3 jit_solution(6373868974499890233)
XLA Ops:
  0.0 1.8 reshape.23
  1.8 0.8 eq.93
  2.6 1.8 fusion.36
  4.4 1.1 copy.37
  5.5 0.8 slice_bitcast_fusion.4
  6.3 0.7 slice_bitcast_fusion.8
  7.1 1.5 collective-permute-start
  8.6 1.0 slice_bitcast_fusion
  9.6 0.8 compare_select_fusion
  10.3 1.0 fusion.42
  11.4 0.9 slice_reduce_fusion.1
  12.3 34.3 %gather_fusion = s32[6144]{0:T(1024)S(1)} fusion(s32[3232]{0:T(1024)S(1)} %get-tuple-element.6, s32[6144]{0:T(1024)S(1)} %broadcast_clamp_fusion), kind=kCustom, calls=%fused_computation | custom fusion | bytes 73728 | tf_op jit(solution)/shard_map/jit(_take)/gather | solution.py:32
  46.7 11.6 %fusion.58 = f32[1408,3232]{1,0:T(8,128)} fusion(f32[3232]{0:T(1024)S(1)} %div.11, s32[3232]{0:T(1024)S(1)} %get-tuple-element.6, s32[3232]{0:T(1024)S(1)} %get-tuple-element.5), kind=kLoop, calls=%fused_computation.2.clone.2 | loop fusion | flops 27303936 | bytes 18241408 | tf_op jit(solution)/shard_map/dot_general | solution.py:49
  58.4 6.5 %collective-permute-start.3 = (f32[495,65]{0,1:T(8,128)S(1)}, f32[495,65]{0,1:T(8,128)S(1)}, u32[]{:S(2)}, u32[]{:S(2)}) collective-permute-start(f32[495,65]{0,1:T(8,128)S(1)} %pad_maximum_fusion.3), channel_id=1, source_target_pairs={{0,240},{1,241},{2,242},{3,243},{4,244},{5,245},{6,246},{7,247},{8... | collective-permute-start | bytes 386108 | tf_op jit(solution)/shard_map/ppermute | solution.py:12
  65.3 93.5 %fusion = f32[1408,1024]{1,0:T(8,128)} fusion(f32[1024]{0:T(1024)S(1)} %copy-done.6, f32[1024]{0:T(1024)S(1)} %bitcast.68, s32[1024]{0:T(1024)S(1)} %bitcast.65, f32[1024]{0:T(1024)S(1)} %bitcast.69, s32[1024]{0:T(1024)S(1)} %bitcast.66, f32[1024]{0:T(1024)S(1)} %bitcast.70, s32[1024]{0:T(1024)S(1)} %bitcast.64, f32[1024]{0:T(1024)S(1)} %bitcast.71, ...), kind=kOutput, calls=%fused_computation.1 | convolution fusion | flops 55978033152 | bytes 24023040 | tf_op jit(solution)/shard_map/dot_general | solution.py:49
  160.4 1.6 slice.179
  161.9 1.0 copy.40
  163.0 3.1 %concatenate.34 = f32[495,1408]{1,0:T(8,128)} concatenate(f32[495,1024]{1,0:T(8,128)S(1)} %reshape.23, f32[495,64]{1,0:T(8,128)S(1)} %pad.26.clone, f32[495,64]{1,0:T(8,128)S(1)} %pad.27.clone, f32[495,64]{1,0:T(8,128)S(1)} %copy.40, f32[495,64]{1,0:T(8,128)S(1)} %copy.41, f32[495,64]{1,0:T(8,128)S(1)} %pad.28.clone, f32[495,64]{1,0:T(8,128)S(1)} %pad.29.clone), dimensions={1} | concatenate | bytes 5575680 | tf_op jit(solution)/shard_map/concatenate | solution.py:79
  166.0 13.0 %fusion.44 = f32[495,1024]{1,0:T(8,128)S(1)} fusion(f32[495,1408]{1,0:T(8,128)} %concatenate.34, f32[1408,1024]{1,0:T(8,128)} %fusion), kind=kOutput, calls=%fused_computation.78 | convolution fusion | flops 8564244480 | bytes 10582528 | tf_op jit(solution)/shard_map/dot_general | solution.py:94
  179.0 1.6 fusion.34
  180.9 4.1 %collective-permute-start.4 = (f32[495,17]{1,0:T(8,128)S(1)}, f32[495,17]{1,0:T(8,128)S(1)}, u32[]{:S(2)}, u32[]{:S(2)}) collective-permute-start(f32[495,17]{1,0:T(8,128)S(1)} %copy.45), channel_id=1, source_target_pairs={{0,1},{1,2},{2,3},{3,4},{4,5},{5,6},{6,7},{7,8},{8,9},{9,10},{10,1... | collective-permute-start | bytes 100988 | tf_op jit(solution)/shard_map/ppermute | solution.py:12
  185.2 0.8 copy.46
  186.2 2.1 collective-permute-done.4
  188.6 6.0 %collective-permute-start.7 = (f32[495,65]{1,0:T(8,128)S(1)}, f32[495,65]{1,0:T(8,128)S(1)}, u32[]{:S(2)}, u32[]{:S(2)}) collective-permute-start(f32[495,65]{1,0:T(8,128)S(1)} %pad_maximum_fusion.1), channel_id=1, source_target_pairs={{0,240},{1,241},{2,242},{3,243},{4,244},{5,245},{6,246},{7,247},{8... | collective-permute-start | bytes 386108 | tf_op jit(solution)/shard_map/ppermute | solution.py:12
  194.5 2.2 collective-permute-done.5
  197.0 1.7 collective-permute-start.6
  198.7 1.2 neg.4
  200.5 9.7 %collective-permute-done.6 = f32[495,65]{1,0:T(8,128)S(1)} collective-permute-done((f32[495,65]{1,0:T(8,128)S(1)}, f32[495,65]{1,0:T(8,128)S(1)}, u32[]{:S(2)}, u32[]{:S(2)}) %collective-permute-start.6) | collective-permute-done | bytes 128732 | tf_op jit(solution)/shard_map/ppermute | solution.py:12
  210.3 3.1 %concatenate.39 = f32[495,1408]{1,0:T(8,128)} concatenate(f32[495,1024]{1,0:T(8,128)S(1)} %fusion.44, f32[495,64]{1,0:T(8,128)S(1)} %pad.30, f32[495,64]{1,0:T(8,128)S(1)} %pad.31, f32[495,64]{1,0:T(8,128)S(1)} %bitcast.60, f32[495,64]{1,0:T(8,128)S(1)} %bitcast.58, f32[495,64]{1,0:T(8,128)S(1)} %pad.32, f32[495,64]{1,0:T(8,128)S(1)} %pad.33), dimensions={1} | concatenate | bytes 5575680 | tf_op jit(solution)/shard_map/concatenate | solution.py:79
  213.4 13.6 %fusion.45 = f32[495,1024]{1,0:T(8,128)} fusion(f32[495,1408]{1,0:T(8,128)} %concatenate.39, f32[1408,1024]{1,0:T(8,128)} %fusion), kind=kOutput, calls=%fused_computation.79 | convolution fusion | flops 8564244480 | bytes 10582528 | tf_op jit(solution)/shard_map/dot_general | solution.py:94
  227.0 1.8 reshape.26
  228.8 1.6 broadcast_multiply_fusion
  (66 shorter events, 3.5 us)
Async XLA Ops:
  2.6 44.0 %copy-start.1 = (s32[384]{0:T(512)}, s32[384]{0:T(512)S(1)}, u32[]{:S(2)}) copy-start(s32[384]{0:T(512)S(1)} %eq.93) | copy-start | bytes 4612
  7.1 51.3 %collective-permute-start = (f32[495,17]{0,1:T(8,128)S(1)}, f32[495,17]{0,1:T(8,128)S(1)}, u32[]{:S(2)}, u32[]{:S(2)}) collective-permute-start(f32[495,17]{0,1:T(8,128)S(1)} %pad_maximum_fusion.4), channel_id=1, source_target_pairs={{0,1},{1,2},{2,3},{3,4},{4,5},{5,6},{6,7},{7,8},{8,9},{9,10},{10,1... | collective-permute-start | bytes 100988 | tf_op jit(solution)/shard_map/ppermute | solution.py:12
  8.6 56.4 %collective-permute-start.1 = (f32[495,17]{0,1:T(8,128)S(1)}, f32[495,17]{0,1:T(8,128)S(1)}, u32[]{:S(2)}, u32[]{:S(2)}) collective-permute-start(f32[495,17]{0,1:T(8,128)S(1)} %pad_maximum_fusion.5), channel_id=1, source_target_pairs={{0,255},{1,0},{2,1},{3,2},{4,3},{5,4},{6,5},{7,6},{8,7},{9,8},{10,... | collective-permute-start | bytes 100988 | tf_op jit(solution)/shard_map/ppermute | solution.py:12
  12.3 34.4 %copy-start = (s32[6,1024]{1,0:T(8,128)S(1)}, s32[6,1024]{1,0:T(8,128)}, u32[]{:S(2)}) copy-start(s32[6,1024]{1,0:T(8,128)} %param.13) | copy-start | bytes 73732
  12.3 34.4 %copy-start.3 = (f32[3232]{0:T(1024)S(1)}, f32[3232]{0:T(1024)}, u32[]{:S(2)}) copy-start(f32[3232]{0:T(1024)} %param.10) | copy-start | bytes 38788
  12.3 34.4 %copy-start.4 = (f32[3232]{0:T(1024)S(1)}, f32[3232]{0:T(1024)}, u32[]{:S(2)}) copy-start(f32[3232]{0:T(1024)} %param.11) | copy-start | bytes 38788
  46.6 18.6 %copy-start.6 = (f32[1024]{0:T(1024)S(1)}, f32[1024]{0:T(1024)}, u32[]{:S(2)}) copy-start(f32[1024]{0:T(1024)} %param.9) | copy-start | bytes 12292
  58.4 100.7 %collective-permute-start.3 = (f32[495,65]{0,1:T(8,128)S(1)}, f32[495,65]{0,1:T(8,128)S(1)}, u32[]{:S(2)}, u32[]{:S(2)}) collective-permute-start(f32[495,65]{0,1:T(8,128)S(1)} %pad_maximum_fusion.3), channel_id=1, source_target_pairs={{0,240},{1,241},{2,242},{3,243},{4,244},{5,245},{6,246},{7,247},{8... | collective-permute-start | bytes 386108 | tf_op jit(solution)/shard_map/ppermute | solution.py:12
  65.0 94.5 %collective-permute-start.2 = (f32[495,65]{0,1:T(8,128)S(1)}, f32[495,65]{0,1:T(8,128)}, u32[]{:S(2)}, u32[]{:S(2)}) collective-permute-start(f32[495,65]{0,1:T(8,128)S(1)} %pad_maximum_fusion.2), channel_id=1, source_target_pairs={{0,16},{1,17},{2,18},{3,19},{4,20},{5,21},{6,22},{7,23},{8,24},{9,... | collective-permute-start | bytes 386108 | tf_op jit(solution)/shard_map/ppermute | solution.py:12
  166.0 13.0 %copy-start.2 = (s32[384]{0:T(512)S(1)}, s32[384]{0:T(512)}, u32[]{:S(2)}) copy-start(s32[384]{0:T(512)} %copy-done.1) | copy-start | bytes 4612
  180.9 7.4 %collective-permute-start.4 = (f32[495,17]{1,0:T(8,128)S(1)}, f32[495,17]{1,0:T(8,128)S(1)}, u32[]{:S(2)}, u32[]{:S(2)}) collective-permute-start(f32[495,17]{1,0:T(8,128)S(1)} %copy.45), channel_id=1, source_target_pairs={{0,1},{1,2},{2,3},{3,4},{4,5},{5,6},{6,7},{7,8},{8,9},{9,10},{10,1... | collective-permute-start | bytes 100988 | tf_op jit(solution)/shard_map/ppermute | solution.py:12
  186.0 10.7 %collective-permute-start.5 = (f32[495,17]{1,0:T(8,128)}, f32[495,17]{1,0:T(8,128)S(1)}, u32[]{:S(2)}, u32[]{:S(2)}) collective-permute-start(f32[495,17]{1,0:T(8,128)} %copy.46), channel_id=1, source_target_pairs={{0,255},{1,0},{2,1},{3,2},{4,3},{5,4},{6,5},{7,6},{8,7},{9,8},{10,... | collective-permute-start | bytes 100988 | tf_op jit(solution)/shard_map/ppermute | solution.py:12
  188.6 11.8 %collective-permute-start.7 = (f32[495,65]{1,0:T(8,128)S(1)}, f32[495,65]{1,0:T(8,128)S(1)}, u32[]{:S(2)}, u32[]{:S(2)}) collective-permute-start(f32[495,65]{1,0:T(8,128)S(1)} %pad_maximum_fusion.1), channel_id=1, source_target_pairs={{0,240},{1,241},{2,242},{3,243},{4,244},{5,245},{6,246},{7,247},{8... | collective-permute-start | bytes 386108 | tf_op jit(solution)/shard_map/ppermute | solution.py:12
  197.0 13.2 %collective-permute-start.6 = (f32[495,65]{1,0:T(8,128)S(1)}, f32[495,65]{1,0:T(8,128)S(1)}, u32[]{:S(2)}, u32[]{:S(2)}) collective-permute-start(f32[495,65]{1,0:T(8,128)S(1)} %pad_maximum_fusion), channel_id=1, source_target_pairs={{0,16},{1,17},{2,18},{3,19},{4,20},{5,21},{6,22},{7,23},{8,24},{9,... | collective-permute-start | bytes 386108 | tf_op jit(solution)/shard_map/ppermute | solution.py:12
  213.4 15.4 %copy-start.5 = (f32[55]{0:T(128)S(1)}, f32[55]{0:T(128)}, u32[]{:S(2)}) copy-start(f32[55]{0:T(128)} %neg.4) | copy-start | bytes 664
where the time goes:
time: 231 us; the launch traced here: 230 us
  matrix products  124 us (54%)
  local copies, waits for them, and re-layouts  56.3 us (24%)
  starting transfers between devices  20.1 us (9%)
  other arithmetic  15.6 us (7%)
  waiting for transfers between devices  14.3 us (6%)
    dot_general x1, matrix products, shards(): jnp.dot(differ, collect, precision=highest, preferred_element_type=jnp.fl...  93.5 us
    gather x2, local copies, waits for them, and re-layouts, shards(): first_end = jnp.take(cells_on_edge[0], edges_on_cell)  34.3 us
    dot_general x2, matrix products, laplacian(): jnp.dot(extended, operator, precision=highest, preferred_element_type=jnp...  26.6 us
    ppermute x8, starting transfers between devices, from_behind(): lax.ppermute(x, axis, [(i, (i + by) % devices) for i in range(devices)])  20.1 us
    ppermute x8, waiting for transfers between devices, from_behind(): lax.ppermute(x, axis, [(i, (i + by) % devices) for i in range(devices)])  14.3 us
    dot_general x1, other arithmetic, shards(): jnp.dot(differ, collect, precision=highest, preferred_element_type=jnp.fl...  11.6 us
    concatenate x2, local copies, waits for them, and re-layouts, extend(): jnp.concatenate([values, widen(from_left, length), widen(from_right, leng...  6.15 us
  transfers between devices with their start and end apart: 8, of which 4 were waited for; matrix products, arithmetic and copies ran while one was open for 64% of the time, Pallas kernels for 0%

commit v1 on v0

v1 whole, which is shorter than its diff:
```python
import functools

import jax
import jax.numpy as jnp
from jax import lax
from jax.experimental import pallas as pl
from jax.experimental.pallas import tpu as pltpu
from jax.sharding import PartitionSpec as P

MESH = pl.DeviceIdType.MESH
F32 = jnp.float32
BF16 = jnp.bfloat16
I32 = jnp.int32

BLOCK_ROW = 16
SIDE = 16
SLOT = 64
CELLS = 1024
HALO = 256
DEPTH = CELLS + HALO
FIELDS = 9
LEVELS = 55
PITCH = 56
ROWS = 512
EDGES = 3232
GROUPS = -(-EDGES // 128)
CORNER_A = CELLS + 192
CORNER_B = CELLS + 224


def dot(a, b):
    return jnp.dot(a, b, preferred_element_type=F32)


def split(x):
    high = x.astype(BF16)
    return high, (x - high.astype(F32)).astype(BF16)


def lanes(shape):
    return lax.broadcasted_iota(I32, shape, 1)


def rows_of(shape):
    return lax.broadcasted_iota(I32, shape, 0)


def kernel(
    field,
    area,
    dv,
    dc,
    ends,
    beside,
    send,
    out,
    xf,
    xh,
    xl,
    select,
    lh,
    ll,
    near,
    coef,
    diag,
    acc,
    halo_h,
    halo_l,
    send_up,
    send_down,
    send_right,
    send_left,
    send_corner,
    got_up,
    got_down,
    got_right,
    got_left,
    got_corner,
    load_sem,
    send_sem,
    recv_sem,
):
    count = lax.axis_size("cells")
    me = lax.axis_index("cells")

    def at(offset):
        return lax.rem(me + (offset + count), count)

    offsets = (1, -1, BLOCK_ROW, -BLOCK_ROW, BLOCK_ROW - 1, 1 - BLOCK_ROW)
    barrier = pltpu.get_barrier_semaphore()
    for offset in offsets:
        pl.semaphore_signal(barrier, inc=1, device_id=(at(offset),), device_id_type=MESH)

    loads = []
    for f in range(FIELDS):
        loads.append(pltpu.make_async_copy(field.at[f], xf.at[f], load_sem.at[f]))
        loads[-1].start()

    lists = send[...]
    wide = (1, 128)
    lane1 = lanes(wide)
    first_cols = jnp.concatenate([lists[2:3], lists[3:4]], axis=1)
    second_cols = jnp.concatenate([lists[0:1], lists[1:2]], axis=1)
    near_cols = jnp.where(lane1 < 16, second_cols, pltpu.roll(second_cols, 80, 1))
    corner_cols = jnp.where(
        lane1 < 96,
        jnp.broadcast_to(lists[4:5, 0:1], wide),
        jnp.broadcast_to(lists[5:6, 0:1], wide),
    )
    second_cols = jnp.where(lane1 < 32, near_cols, jnp.where(lane1 < 64, -1, corner_cols))
    columns = jnp.concatenate([first_cols, second_cols], axis=1)

    def fill_select(i, carry):
        at_row = pl.multiple_of(i * 16, 16)
        ids = rows_of((16, HALO)) + at_row
        select[pl.ds(at_row, 16), :] = jnp.where(ids == columns, 1.0, 0.0).astype(BF16)
        return carry

    lax.fori_loop(0, CELLS // 16, fill_select, 0, unroll=4)

    pad = jnp.zeros((1, CELLS), F32)
    for f in range(FIELDS):
        loads[f].wait()
        acc[pl.ds(f * PITCH, PITCH), :] = jnp.concatenate([xf[f], pad], axis=0)
    acc[pl.ds(FIELDS * PITCH, ROWS - FIELDS * PITCH), :] = jnp.zeros(
        (ROWS - FIELDS * PITCH, CELLS), F32
    )
    high, low = split(acc[...])
    xh[...] = high
    xl[...] = low

    lane = lanes((256, 128))

    def exchange(k):
        picked = dot(xh[...], select[...]) + dot(xl[...], select[...])
        top = picked[:256, :128]
        low_half = picked[256:, :128]
        send_up[k] = jnp.where(lane < 64, top, pltpu.roll(low_half, 64, 1))
        send_down[k] = jnp.where(lane < 64, pltpu.roll(top, 64, 1), low_half)
        rest = picked[:, 128:]
        group = lanes((64, 128)) // 16
        right = rest[0:64]
        left = pltpu.roll(rest[0:64], 112, 1)
        for g in range(1, 8):
            part = rest[64 * g : 64 * g + 64]
            right = jnp.where(group == g, pltpu.roll(part, 16 * g, 1), right)
            left = jnp.where(group == g, part if g == 1 else pltpu.roll(part, 16 * g - 16, 1), left)
        send_right[k] = right
        send_left[k] = left
        lane32 = lanes((32, 128))
        own = (lane32 >= 64) & ((lane32 & 31) == rows_of((32, 128)))
        folded = [
            jnp.sum(jnp.where(own, rest[32 * g : 32 * g + 32], 0.0), axis=0, keepdims=True)
            for g in range(16)
        ]
        send_corner[k] = jnp.concatenate(folded, axis=0)
        if k == 0:
            pl.semaphore_wait(barrier, 6)
        plan = (
            (send_up, got_up, None, offsets[2]),
            (send_down, got_down, None, offsets[3]),
            (send_right, got_right, None, offsets[0]),
            (send_left, got_left, None, offsets[1]),
            (send_corner, got_corner, 0, offsets[4]),
            (send_corner, got_corner, 1, offsets[5]),
        )
        copies = []
        for i, (src, dst, which, offset) in enumerate(plan):
            copies.append(
                pltpu.make_async_remote_copy(
                    src_ref=src.at[k],
                    dst_ref=dst.at[k] if which is None else dst.at[k, which],
                    send_sem=send_sem.at[k, i],
                    recv_sem=recv_sem.at[k, i],
                    device_id=(at(offset),),
                    device_id_type=MESH,
                )
            )
            copies[-1].start()
        return copies

    def receive(k, copies):
        for copy in copies:
            copy.wait_recv()
        up = got_up[k]
        down = got_down[k]
        halo_top = jnp.where(lane < 64, up, pltpu.roll(down, 64, 1))
        halo_low = jnp.where(lane < 64, pltpu.roll(up, 64, 1), down)
        for part, start in ((halo_top, 0), (halo_low, 256)):
            high, low = split(part)
            halo_h[pl.ds(start, 256), 0:128] = high
            halo_l[pl.ds(start, 256), 0:128] = low
        right = got_right[k]
        left = got_left[k]
        corner_a = got_corner[k, 0]
        corner_b = got_corner[k, 1]
        lane64 = lanes((64, 128))
        own = (lane64 & 31) == (rows_of((64, 128)) & 31)
        upper = rows_of((64, 128)) < 32
        lane2 = lanes((2, 128))
        for g in range(8):
            corners = jnp.where(lane2 < 96, corner_a[2 * g : 2 * g + 2], corner_b[2 * g : 2 * g + 2])
            spread = jnp.where(
                upper,
                jnp.broadcast_to(corners[0:1], (64, 128)),
                jnp.broadcast_to(corners[1:2], (64, 128)),
            )
            spread = jnp.where(own, spread, 0.0)
            from_left = right if g == 0 else pltpu.roll(right, 128 - 16 * g, 1)
            from_right = left if g == 1 else pltpu.roll(left, (144 - 16 * g) % 128, 1)
            part = jnp.where(
                lane64 < 16,
                from_left,
                jnp.where(lane64 < 32, from_right, jnp.where(lane64 < 64, 0.0, spread)),
            )
            high, low = split(part)
            halo_h[pl.ds(64 * g, 64), 128:256] = high
            halo_l[pl.ds(64 * g, 64), 128:256] = low

    copies_a = exchange(0)

    packed = []
    weights = []
    for r in range(GROUPS):
        width = min(128, EDGES - 128 * r)
        where = slice(128 * r, 128 * r + width)
        both = ends[0:1, where] | (ends[1:2, where] << 11)
        ratio = dv[0:1, where] / dc[0:1, where]
        if width < 128:
            both = jnp.concatenate([both, jnp.zeros((1, 128 - width), I32)], axis=1)
            ratio = jnp.concatenate([ratio, jnp.zeros((1, 128 - width), F32)], axis=1)
        packed.append(jnp.broadcast_to(both, (8, 128)))
        weights.append(jnp.broadcast_to(ratio, (8, 128)))
    edge_ids = jnp.concatenate([beside[...], jnp.zeros((2, CELLS), I32)], axis=0)
    tile = (8, 128)
    valid = rows_of(tile) < 6
    for t in range(CELLS // 128):
        cols = slice(128 * t, 128 * t + 128)
        ids = edge_ids[:, cols]
        group = ids >> 7
        within = ids & 127
        both = jnp.zeros(tile, I32)
        ratio = jnp.zeros(tile, F32)
        for r in range(GROUPS):
            here = group == r
            both = jnp.where(here, jnp.take_along_axis(packed[r], within, axis=1), both)
            ratio = jnp.where(here, jnp.take_along_axis(weights[r], within, axis=1), ratio)
        end0 = both & 2047
        end1 = both >> 11
        other = jnp.where(end0 == lanes(tile) + 128 * t, end1, end0)
        beyond = other - CELLS
        slot = beyond >> 6
        place = beyond & 63
        start = jnp.where(
            slot == 2,
            CELLS,
            jnp.where(
                slot == 3,
                CELLS + 64,
                jnp.where(
                    slot == 0,
                    CELLS + 128,
                    jnp.where(slot == 1, CELLS + 144, jnp.where(slot == 4, CORNER_A, CORNER_B)),
                ),
            ),
        )
        other = jnp.where(other < CELLS, other, start + place)
        near[:, cols] = jnp.where(valid, other, -1)
        factor = jnp.where(valid, ratio / area[0:1, cols], 0.0)
        high, low = split(factor)
        factor = high.astype(F32) + low.astype(F32)
        coef[:, cols] = factor
        diag[0:1, cols] = jnp.sum(factor, axis=0, keepdims=True)

    for t in range(CELLS // 128):
        cols = slice(128 * t, 128 * t + 128)
        nears = [jnp.broadcast_to(near[j : j + 1, cols], (16, 128)) for j in range(6)]
        coefs = [jnp.broadcast_to(coef[j : j + 1, cols], (16, 128)) for j in range(6)]

        def put(at_row, ids, cols=cols, nears=nears, coefs=coefs):
            value = jnp.where(ids == nears[0], coefs[0], 0.0)
            for j in range(1, 6):
                value = jnp.where(ids == nears[j], coefs[j], value)
            high, low = split(value)
            lh[pl.ds(at_row, 16), cols] = high
            ll[pl.ds(at_row, 16), cols] = low

        def fill(i, carry, put=put):
            at_row = pl.multiple_of(i * 16, 16)
            put(at_row, rows_of((16, 128)) + at_row)
            return carry

        lax.fori_loop(0, CORNER_A // 16, fill, 0, unroll=4)
        for at_row in range(CORNER_A, DEPTH, 16):
            put(at_row, jnp.full((16, 128), CORNER_A if at_row < CORNER_B else CORNER_B, I32))

    tiles = [slice(256 * n, 256 * n + 256) for n in range(CELLS // 256)]

    def own_part():
        for cols in tiles:
            a = dot(xh[...], lh[0:CELLS, cols])
            a += dot(xh[...], ll[0:CELLS, cols])
            a += dot(xl[...], lh[0:CELLS, cols])
            acc[:, cols] = a - diag[0:1, cols] * acc[:, cols]

    def halo_part(cols):
        a = dot(halo_h[...], lh[CELLS:DEPTH, cols])
        a += dot(halo_h[...], ll[CELLS:DEPTH, cols])
        a += dot(halo_l[...], lh[CELLS:DEPTH, cols])
        return acc[:, cols] + a

    own_part()
    receive(0, copies_a)
    for cols in tiles:
        value = halo_part(cols)
        acc[:, cols] = value
        high, low = split(value)
        xh[:, cols] = high
        xl[:, cols] = low
    copies_b = exchange(1)
    own_part()
    receive(1, copies_b)
    for cols in tiles:
        value = halo_part(cols)
        for f in range(FIELDS):
            out[f, :, cols] = value[f * PITCH : f * PITCH + LEVELS]
    for copy in copies_a + copies_b:
        copy.wait_send()


def shards(
    field, cell_area, dv_edge, dc_edge, cells_on_edge, edges_on_cell, send_cells, level_coef
):
    vmem = pl.BlockSpec(memory_space=pltpu.VMEM)
    second = pl.pallas_call(
        kernel,
        out_shape=jax.ShapeDtypeStruct(field.shape, F32),
        in_specs=[pl.BlockSpec(memory_space=pl.ANY)] + [vmem] * 6,
        out_specs=vmem,
        scratch_shapes=[
            pltpu.VMEM((FIELDS, LEVELS, CELLS), F32),
            pltpu.VMEM((ROWS, CELLS), BF16),
            pltpu.VMEM((ROWS, CELLS), BF16),
            pltpu.VMEM((CELLS, HALO), BF16),
            pltpu.VMEM((DEPTH, CELLS), BF16),
            pltpu.VMEM((DEPTH, CELLS), BF16),
            pltpu.VMEM((8, CELLS), I32),
            pltpu.VMEM((8, CELLS), F32),
            pltpu.VMEM((1, CELLS), F32),
            pltpu.VMEM((ROWS, CELLS), F32),
            pltpu.VMEM((ROWS, HALO), BF16),
            pltpu.VMEM((ROWS, HALO), BF16),
            pltpu.VMEM((2, 256, 128), F32),
            pltpu.VMEM((2, 256, 128), F32),
            pltpu.VMEM((2, 64, 128), F32),
            pltpu.VMEM((2, 64, 128), F32),
            pltpu.VMEM((2, 16, 128), F32),
            pltpu.VMEM((2, 256, 128), F32),
            pltpu.VMEM((2, 256, 128), F32),
            pltpu.VMEM((2, 64, 128), F32),
            pltpu.VMEM((2, 64, 128), F32),
            pltpu.VMEM((2, 2, 16, 128), F32),
            pltpu.SemaphoreType.DMA((FIELDS,)),
            pltpu.SemaphoreType.DMA((2, 6)),
            pltpu.SemaphoreType.DMA((2, 6)),
        ],
        compiler_params=pltpu.CompilerParams(
            collective_id=0, has_side_effects=True, vmem_limit_bytes=48 * 1024 * 1024
        ),
        name="diffusion",
    )(
        field,
        cell_area.reshape(1, -1),
        dv_edge.reshape(1, -1),
        dc_edge.reshape(1, -1),
        cells_on_edge,
        edges_on_cell,
        send_cells,
    )
    return -level_coef[None, :, None] * second


def solution(mesh):
    return jax.shard_map(
        shards,
        mesh=mesh,
        in_specs=(
            P(None, None, "cells"),
            P("cells"),
            P("cells"),
            P("cells"),
            P(None, "cells"),
            P(None, "cells"),
            P(None, "cells"),
            P(),
        ),
        out_specs=P(None, None, "cells"),
        check_vma=False,
    )
```

time: 231 us -> 39.3 us (0.17)
  the two profiles are of different devices: /device:TPU:27 before, /device:TPU:1 now
where the time goes in v1:
time: 39.3 us; the launch traced here: 38.9 us
  Pallas kernels  31.4 us (80%)
  local copies, waits for them, and re-layouts  5.91 us (15%)
  other arithmetic  1.6 us (4%)
    pallas_call x1, Pallas kernels, shards(): pl.pallas_call(kernel, out_shape=jax.ShapeDtypeStruct(field.shape, F32),...  31.4 us
    unnamed x12, local copies, waits for them, and re-layouts  4.45 us
    mul x1, other arithmetic, shards(): return -level_coef[None, :, None] * second  1.6 us

profile of v1, /device:TPU:1, one launch (start us, length us, event | category | flops | bytes accessed | tf_op | source)
XLA Modules:
  0.0 38.9 jit_solution(11066972870699017693)
XLA Ops:
  0.0 0.7 %reshape.12.dv = f32[1,3232]{1,0:T(1,128)S(1)} reshape(f32[3232]{0:T(1024)} %param.10) | data formatting | bytes 25856 | tf_op jit(solution)/shard_map/reshape | solution.py:374
  0.7 0.7 %reshape.13.dc = f32[1,3232]{1,0:T(1,128)S(1)} reshape(f32[3232]{0:T(1024)} %param.11) | data formatting | bytes 25856 | tf_op jit(solution)/shard_map/reshape | solution.py:375
  1.5 0.0 copy-start
  1.5 1.6 %copy-done = f32[9,55,1024]{2,1,0:T(8,128)S(1)} copy-done((f32[9,55,1024]{2,1,0:T(8,128)S(1)}, f32[9,55,1024]{2,1,0:T(8,128)}, u32[]{:S(2)}) %copy-start) | copy-done | bytes 2027544
  3.0 0.0 copy-start.1
  3.0 0.8 %copy-done.1 = s32[6,1024]{1,0:T(8,128)S(1)} copy-done((s32[6,1024]{1,0:T(8,128)S(1)}, s32[6,1024]{1,0:T(8,128)}, u32[]{:S(2)}) %copy-start.1) | copy-done | bytes 24600
  3.8 0.0 copy-start.2
  3.8 0.7 %copy-done.2 = s32[2,3232]{1,0:T(2,128)S(1)} copy-done((s32[2,3232]{1,0:T(2,128)S(1)}, s32[2,3232]{1,0:T(2,128)}, u32[]{:S(2)}) %copy-start.2) | copy-done | bytes 25880
  4.5 0.0 copy-start.3
  4.5 0.7 %copy-done.3 = f32[1024]{0:T(1024)S(1)} copy-done((f32[1024]{0:T(1024)S(1)}, f32[1024]{0:T(1024)}, u32[]{:S(2)}) %copy-start.3) | copy-done | bytes 4120
  5.2 0.0 copy-start.4
  5.2 0.7 %copy-done.4 = s32[6,64]{1,0:T(8,128)S(1)} copy-done((s32[6,64]{1,0:T(8,128)S(1)}, s32[6,64]{1,0:T(8,128)}, u32[]{:S(2)}) %copy-start.4) | copy-done | bytes 1560
  5.9 0.0 copy-start.5
  5.9 31.4 %diffusion.1 = f32[9,55,1024]{2,1,0:T(8,128)S(1)} custom-call(f32[9,55,1024]{2,1,0:T(8,128)S(1)} %copy-done, f32[1,1024]{1,0:T(1,128)S(1)} %bitcast.1, f32[1,3232]{1,0:T(1,128)S(1)} %reshape.12.dv, f32[1,3232]{1,0:T(1,128)S(1)} %reshape.13.dc, s32[2,3232]{1,0:T(2,128)S(1)} %copy-done.2, s32[6,1024]{1,0:T(8,128)S(1)} %copy-done.1, s32[6,64]{1,0:T(8,128)S(1)} %copy-done.4), custom_call_target="tpu_custom_call" | custom-call | tf_op jit(solution)/shard_map/diffusion/pallas_call | solution.py:335
  37.3 0.0 copy-done.5
  37.3 1.6 %broadcast_multiply_fusion = f32[9,55,1024]{2,1,0:T(8,128)} fusion(f32[9,55,1024]{2,1,0:T(8,128)S(1)} %diffusion.1, f32[55]{0:T(128)S(1)} %neg.4), kind=kLoop, calls=%fused_computation | loop fusion | flops 506880 | bytes 4055260 | tf_op jit(solution)/shard_map/mul | solution.py:380
  (1 shorter events, 0.0 us)
Async XLA Ops:
  1.5 1.6 %copy-start = (f32[9,55,1024]{2,1,0:T(8,128)S(1)}, f32[9,55,1024]{2,1,0:T(8,128)}, u32[]{:S(2)}) copy-start(f32[9,55,1024]{2,1,0:T(8,128)} %field.1) | copy-start | bytes 6082564
  3.0 0.8 %copy-start.1 = (s32[6,1024]{1,0:T(8,128)S(1)}, s32[6,1024]{1,0:T(8,128)}, u32[]{:S(2)}) copy-start(s32[6,1024]{1,0:T(8,128)} %beside.1) | copy-start | bytes 73732
  3.8 0.7 %copy-start.2 = (s32[2,3232]{1,0:T(2,128)S(1)}, s32[2,3232]{1,0:T(2,128)}, u32[]{:S(2)}) copy-start(s32[2,3232]{1,0:T(2,128)} %ends.1) | copy-start | bytes 77572
  4.5 0.7 %copy-start.3 = (f32[1024]{0:T(1024)S(1)}, f32[1024]{0:T(1024)}, u32[]{:S(2)}) copy-start(f32[1024]{0:T(1024)} %param.9) | copy-start | bytes 12292
  5.2 0.7 %copy-start.4 = (s32[6,64]{1,0:T(8,128)S(1)}, s32[6,64]{1,0:T(8,128)}, u32[]{:S(2)}) copy-start(s32[6,64]{1,0:T(8,128)} %send.1) | copy-start | bytes 4612
  5.9 31.4 %copy-start.5 = (f32[55]{0:T(128)S(1)}, f32[55]{0:T(128)}, u32[]{:S(2)}) copy-start(f32[55]{0:T(128)} %param.15) | copy-start | bytes 664

commit v2 on v1

v2 whole, which is shorter than its diff:
```python
import functools

import jax
import jax.numpy as jnp
from jax import lax
from jax.experimental import pallas as pl
from jax.experimental.pallas import tpu as pltpu
from jax.sharding import PartitionSpec as P

MESH = pl.DeviceIdType.MESH
F32 = jnp.float32
BF16 = jnp.bfloat16
I32 = jnp.int32

BLOCK_ROW = 16
SIDE = 16
SLOT = 64
CELLS = 1024
HALO = 256
FIELDS = 9
LEVELS = 55
PITCH = 56
ROWS = 512
CHUNKS = 2
CHUNK = ROWS // CHUNKS
EDGES = 3232
GROUPS = -(-EDGES // 128)
CORNER_A = CELLS + 192
CORNER_B = CELLS + 224


def dot(a, b):
    return jnp.dot(a, b, preferred_element_type=F32)


def split(x):
    high = x.astype(BF16)
    return high, (x - high.astype(F32)).astype(BF16)


def lanes(shape):
    return lax.broadcasted_iota(I32, shape, 1)


def rows_of(shape):
    return lax.broadcasted_iota(I32, shape, 0)


def kernel(
    field,
    area_in,
    dv_in,
    dc_in,
    ends_in,
    beside_in,
    send_in,
    acc,
    halo_h,
    halo_l,
    rim_h,
    rim_l,
    area,
    dv,
    dc,
    ends,
    beside,
    send,
    xf,
    xh,
    xl,
    select,
    lh,
    ll,
    near,
    coef,
    diag,
    send_up,
    send_down,
    send_right,
    send_left,
    send_corner,
    got_up,
    got_down,
    got_right,
    got_left,
    got_corner,
    load_sem,
    send_sem,
    recv_sem,
):
    count = lax.axis_size("cells")
    me = lax.axis_index("cells")

    def at(offset):
        return lax.rem(me + (offset + count), count)

    offsets = (1, -1, BLOCK_ROW, -BLOCK_ROW, BLOCK_ROW - 1, 1 - BLOCK_ROW)
    barrier = pltpu.get_barrier_semaphore()
    for offset in offsets:
        pl.semaphore_signal(barrier, inc=1, device_id=(at(offset),), device_id_type=MESH)

    def load(i, src, dst):
        copy = pltpu.make_async_copy(src, dst, load_sem.at[i])
        copy.start()
        return copy

    list_load = load(FIELDS, send_in, send)
    loads = [load(f, field.at[f], xf.at[f]) for f in range(FIELDS)]
    table_loads = [
        load(FIELDS + 1 + i, src, dst)
        for i, (src, dst) in enumerate(
            ((beside_in, beside), (ends_in, ends), (dv_in, dv), (dc_in, dc), (area_in, area))
        )
    ]

    list_load.wait()
    lists = send[...]
    wide = (1, 128)
    lane1 = lanes(wide)
    first_cols = jnp.concatenate([lists[2:3], lists[3:4]], axis=1)
    second_cols = jnp.concatenate([lists[0:1], lists[1:2]], axis=1)
    near_cols = jnp.where(lane1 < 16, second_cols, pltpu.roll(second_cols, 80, 1))
    corner_cols = jnp.where(
        lane1 < 96,
        jnp.broadcast_to(lists[4:5, 0:1], wide),
        jnp.broadcast_to(lists[5:6, 0:1], wide),
    )
    second_cols = jnp.where(lane1 < 32, near_cols, jnp.where(lane1 < 64, -1, corner_cols))
    columns = jnp.concatenate([first_cols, second_cols], axis=1)

    def fill_select(i, carry):
        at_row = pl.multiple_of(i * 16, 16)
        ids = rows_of((16, HALO)) + at_row
        select[pl.ds(at_row, 16), :] = jnp.where(ids == columns, 1.0, 0.0).astype(BF16)
        return carry

    lax.fori_loop(0, CELLS // 16, fill_select, 0, unroll=8)

    half = CHUNK // 2
    part = CHUNK // 8
    corner_rows = CHUNK // 32

    def exchange(k, h):
        here = pl.ds(h * CHUNK, CHUNK)
        picked = dot(xh[here, :], select[...]) + dot(xl[here, :], select[...])
        lane = lanes((half, 128))
        top = picked[:half, :128]
        low_half = picked[half:, :128]
        send_up[k, h] = jnp.where(lane < 64, top, pltpu.roll(low_half, 64, 1))
        send_down[k, h] = jnp.where(lane < 64, pltpu.roll(top, 64, 1), low_half)
        rest = picked[:, 128:]
        group = lanes((part, 128)) // 16
        right = rest[0:part]
        left = pltpu.roll(rest[0:part], 112, 1)
        for g in range(1, 8):
            piece = rest[part * g : part * g + part]
            right = jnp.where(group == g, pltpu.roll(piece, 16 * g, 1), right)
            left = jnp.where(group == g, piece if g == 1 else pltpu.roll(piece, 16 * g - 16, 1), left)
        send_right[k, h] = right
        send_left[k, h] = left
        lane32 = lanes((32, 128))
        own = (lane32 >= 64) & ((lane32 & 31) == rows_of((32, 128)))
        folded = [
            jnp.sum(jnp.where(own, rest[32 * g : 32 * g + 32], 0.0), axis=0, keepdims=True)
            for g in range(corner_rows)
        ]
        send_corner[k, h] = jnp.concatenate(folded, axis=0)
        if k == 0 and h == 0:
            pl.semaphore_wait(barrier, 6)
        plan = (
            (send_up, got_up.at[k, h], offsets[2]),
            (send_down, got_down.at[k, h], offsets[3]),
            (send_right, got_right.at[k, h], offsets[0]),
            (send_left, got_left.at[k, h], offsets[1]),
            (send_corner, got_corner.at[k, h, 0], offsets[4]),
            (send_corner, got_corner.at[k, h, 1], offsets[5]),
        )
        copies = []
        for i, (src, dst, offset) in enumerate(plan):
            copies.append(
                pltpu.make_async_remote_copy(
                    src_ref=src.at[k, h],
                    dst_ref=dst,
                    send_sem=send_sem.at[k, h, i],
                    recv_sem=recv_sem.at[k, h, i],
                    device_id=(at(offset),),
                    device_id_type=MESH,
                )
            )
            copies[-1].start()
        return copies

    def receive(k, h, copies):
        for copy in copies:
            copy.wait_recv()
        lane = lanes((half, 128))
        up = got_up[k, h]
        down = got_down[k, h]
        halo_top = jnp.where(lane < 64, up, pltpu.roll(down, 64, 1))
        halo_low = jnp.where(lane < 64, pltpu.roll(up, 64, 1), down)
        for piece, start in ((halo_top, 0), (halo_low, half)):
            high, low = split(piece)
            halo_h[pl.ds(h * CHUNK + start, half), 0:128] = high
            halo_l[pl.ds(h * CHUNK + start, half), 0:128] = low
        right = got_right[k, h]
        left = got_left[k, h]
        corner_a = got_corner[k, h, 0]
        corner_b = got_corner[k, h, 1]
        shape = (part, 128)
        lane = lanes(shape)
        own = (lane & 31) == rows_of(shape)
        corners = jnp.where(lanes((corner_rows, 128)) < 96, corner_a, corner_b)
        for g in range(8):
            spread = jnp.where(own, jnp.broadcast_to(corners[g : g + 1], shape), 0.0)
            from_left = right if g == 0 else pltpu.roll(right, 128 - 16 * g, 1)
            from_right = left if g == 1 else pltpu.roll(left, (144 - 16 * g) % 128, 1)
            piece = jnp.where(
                lane < 16,
                from_left,
                jnp.where(lane < 32, from_right, jnp.where(lane < 64, 0.0, spread)),
            )
            high, low = split(piece)
            halo_h[pl.ds(h * CHUNK + part * g, part), 128:256] = high
            halo_l[pl.ds(h * CHUNK + part * g, part), 128:256] = low

    pad = jnp.zeros((PITCH - LEVELS, CELLS), F32)
    acc[FIELDS * PITCH : ROWS, :] = jnp.zeros((ROWS - FIELDS * PITCH, CELLS), F32)
    copies_a = []
    waited = 0
    for h in range(CHUNKS):
        while waited < FIELDS and waited * PITCH < (h + 1) * CHUNK:
            loads[waited].wait()
            acc[pl.ds(waited * PITCH, PITCH), :] = jnp.concatenate([xf[waited], pad], axis=0)
            waited += 1
        here = pl.ds(h * CHUNK, CHUNK)
        high, low = split(acc[here, :])
        xh[here, :] = high
        xl[here, :] = low
        copies_a.append(exchange(0, h))

    for copy in table_loads:
        copy.wait()
    packed = []
    weights = []
    for r in range(GROUPS):
        width = min(128, EDGES - 128 * r)
        where = slice(128 * r, 128 * r + width)
        both = ends[0:1, where] | (ends[1:2, where] << 11)
        ratio = (dv[where] / dc[where]).reshape(1, width)
        if width < 128:
            both = jnp.concatenate([both, jnp.zeros((1, 128 - width), I32)], axis=1)
            ratio = jnp.concatenate([ratio, jnp.zeros((1, 128 - width), F32)], axis=1)
        packed.append(jnp.broadcast_to(both, (8, 128)))
        weights.append(jnp.broadcast_to(ratio, (8, 128)))
    edge_ids = jnp.concatenate([beside[...], jnp.zeros((2, CELLS), I32)], axis=0)
    tile = (8, 128)
    valid = rows_of(tile) < 6
    for t in range(CELLS // 128):
        cols = slice(128 * t, 128 * t + 128)
        ids = edge_ids[:, cols]
        group = ids >> 7
        within = ids & 127
        both = jnp.zeros(tile, I32)
        ratio = jnp.zeros(tile, F32)
        for r in range(GROUPS):
            here = group == r
            both = jnp.where(here, jnp.take_along_axis(packed[r], within, axis=1), both)
            ratio = jnp.where(here, jnp.take_along_axis(weights[r], within, axis=1), ratio)
        end0 = both & 2047
        end1 = both >> 11
        other = jnp.where(end0 == lanes(tile) + 128 * t, end1, end0)
        beyond = other - CELLS
        slot = beyond >> 6
        place = beyond & 63
        start = jnp.where(
            slot == 2,
            CELLS,
            jnp.where(
                slot == 3,
                CELLS + 64,
                jnp.where(
                    slot == 0,
                    CELLS + 128,
                    jnp.where(slot == 1, CELLS + 144, jnp.where(slot == 4, CORNER_A, CORNER_B)),
                ),
            ),
        )
        other = jnp.where(other < CELLS, other, start + place)
        near[:, cols] = jnp.where(valid, other, -1)
        factor = jnp.where(valid, ratio / area[cols].reshape(1, 128), 0.0)
        high, low = split(factor)
        factor = high.astype(F32) + low.astype(F32)
        coef[:, cols] = factor
        diag[0:1, cols] = jnp.sum(factor, axis=0, keepdims=True)

    for t in range(CELLS // 128):
        cols = slice(128 * t, 128 * t + 128)
        nears = [jnp.broadcast_to(near[j : j + 1, cols], (16, 128)) for j in range(6)]
        coefs = [jnp.broadcast_to(coef[j : j + 1, cols], (16, 128)) for j in range(6)]

        def put(high_ref, low_ref, at_row, ids, cols=cols, nears=nears, coefs=coefs):
            value = jnp.where(ids == nears[0], coefs[0], 0.0)
            for j in range(1, 6):
                value = jnp.where(ids == nears[j], coefs[j], value)
            high, low = split(value)
            high_ref[pl.ds(at_row, 16), cols] = high
            low_ref[pl.ds(at_row, 16), cols] = low

        def fill(i, carry, put=put):
            at_row = pl.multiple_of(i * 16, 16)
            put(lh, ll, at_row, rows_of((16, 128)) + at_row)
            return carry

        lax.fori_loop(0, CELLS // 16, fill, 0, unroll=8)
        for at_row in range(0, HALO, 16):
            ids = rows_of((16, 128)) + (CELLS + at_row)
            if CELLS + at_row >= CORNER_A:
                corner = CORNER_A if CELLS + at_row < CORNER_B else CORNER_B
                ids = jnp.full((16, 128), corner, I32)
            put(rim_h, rim_l, at_row, ids)

    tiles = [slice(256 * n, 256 * n + 256) for n in range(CELLS // 256)]

    def own_part():
        for cols in tiles:
            a = dot(xh[...], lh[:, cols])
            a += dot(xh[...], ll[:, cols])
            a += dot(xl[...], lh[:, cols])
            acc[:, cols] = a - diag[0:1, cols] * acc[:, cols]

    own_part()
    copies_b = []
    for h in range(CHUNKS):
        receive(0, h, copies_a[h])
        here = pl.ds(h * CHUNK, CHUNK)
        for cols in tiles:
            a = dot(halo_h[here, :], rim_h[:, cols])
            a += dot(halo_h[here, :], rim_l[:, cols])
            a += dot(halo_l[here, :], rim_h[:, cols])
            value = acc[here, cols] + a
            acc[here, cols] = value
            high, low = split(value)
            xh[here, cols] = high
            xl[here, cols] = low
        copies_b.append(exchange(1, h))
    own_part()
    for h in range(CHUNKS):
        receive(1, h, copies_b[h])
    for h in range(CHUNKS):
        for copy in copies_a[h] + copies_b[h]:
            copy.wait_send()


def finish(acc, halo_h, halo_l, rim_h, rim_l, level, out, result, sem):
    spread = jnp.broadcast_to(level[...], (LEVELS, LEVELS))
    on_diagonal = lanes((LEVELS, LEVELS)) == rows_of((LEVELS, LEVELS))
    scale = -jnp.sum(jnp.where(on_diagonal, spread, 0.0), axis=1, keepdims=True)
    copies = []
    for n in range(CELLS // 256):
        cols = slice(256 * n, 256 * n + 256)
        a = dot(halo_h[...], rim_h[:, cols])
        a += dot(halo_h[...], rim_l[:, cols])
        a += dot(halo_l[...], rim_h[:, cols])
        value = acc[:, cols] + a
        for f in range(FIELDS):
            result[f, :, cols] = value[f * PITCH : f * PITCH + LEVELS] * scale
        copies.append(
            pltpu.make_async_copy(result.at[:, :, cols], out.at[:, :, cols], sem.at[n])
        )
        copies[-1].start()
    for copy in copies:
        copy.wait()


def shards(
    field, cell_area, dv_edge, dc_edge, cells_on_edge, edges_on_cell, send_cells, level_coef
):
    vmem = pl.BlockSpec(memory_space=pltpu.VMEM)
    hbm = pl.BlockSpec(memory_space=pltpu.HBM)
    half = CHUNK // 2
    part = CHUNK // 8
    corner_rows = CHUNK // 32
    ends = (2, CHUNKS)
    parts = pl.pallas_call(
        kernel,
        out_shape=[
            jax.ShapeDtypeStruct((ROWS, CELLS), F32),
            jax.ShapeDtypeStruct((ROWS, HALO), BF16),
            jax.ShapeDtypeStruct((ROWS, HALO), BF16),
            jax.ShapeDtypeStruct((HALO, CELLS), BF16),
            jax.ShapeDtypeStruct((HALO, CELLS), BF16),
        ],
        in_specs=[hbm] * 7,
        out_specs=[vmem] * 5,
        scratch_shapes=[
            pltpu.VMEM((CELLS,), F32),
            pltpu.VMEM((EDGES,), F32),
            pltpu.VMEM((EDGES,), F32),
            pltpu.VMEM((2, EDGES), I32),
            pltpu.VMEM((6, CELLS), I32),
            pltpu.VMEM((6, SLOT), I32),
            pltpu.VMEM((FIELDS, LEVELS, CELLS), F32),
            pltpu.VMEM((ROWS, CELLS), BF16),
            pltpu.VMEM((ROWS, CELLS), BF16),
            pltpu.VMEM((CELLS, HALO), BF16),
            pltpu.VMEM((CELLS, CELLS), BF16),
            pltpu.VMEM((CELLS, CELLS), BF16),
            pltpu.VMEM((8, CELLS), I32),
            pltpu.VMEM((8, CELLS), F32),
            pltpu.VMEM((1, CELLS), F32),
            pltpu.VMEM((*ends, half, 128), F32),
            pltpu.VMEM((*ends, half, 128), F32),
            pltpu.VMEM((*ends, part, 128), F32),
            pltpu.VMEM((*ends, part, 128), F32),
            pltpu.VMEM((*ends, corner_rows, 128), F32),
            pltpu.VMEM((*ends, half, 128), F32),
            pltpu.VMEM((*ends, half, 128), F32),
            pltpu.VMEM((*ends, part, 128), F32),
            pltpu.VMEM((*ends, part, 128), F32),
            pltpu.VMEM((*ends, 2, corner_rows, 128), F32),
            pltpu.SemaphoreType.DMA((FIELDS + 6,)),
            pltpu.SemaphoreType.DMA((*ends, 6)),
            pltpu.SemaphoreType.DMA((*ends, 6)),
        ],
        compiler_params=pltpu.CompilerParams(
            collective_id=0, has_side_effects=True, vmem_limit_bytes=40 * 1024 * 1024
        ),
        name="diffusion",
    )(
        *(
            pltpu.with_memory_space_constraint(x, pltpu.HBM)
            for x in (
                field, cell_area, dv_edge, dc_edge, cells_on_edge, edges_on_cell, send_cells
            )
        )
    )
    return pl.pallas_call(
        finish,
        out_shape=jax.ShapeDtypeStruct(field.shape, F32),
        in_specs=[vmem] * 6,
        out_specs=hbm,
        scratch_shapes=[
            pltpu.VMEM((FIELDS, LEVELS, CELLS), F32),
            pltpu.SemaphoreType.DMA((CELLS // 256,)),
        ],
        compiler_params=pltpu.CompilerParams(vmem_limit_bytes=40 * 1024 * 1024),
        name="finish",
    )(*parts, level_coef.reshape(1, -1))


def solution(mesh):
    return jax.shard_map(
        shards,
        mesh=mesh,
        in_specs=(
            P(None, None, "cells"),
            P("cells"),
            P("cells"),
            P("cells"),
            P(None, "cells"),
            P(None, "cells"),
            P(None, "cells"),
            P(),
        ),
        out_specs=P(None, None, "cells"),
        check_vma=False,
    )
```

time: 39.3 us -> 29.4 us (0.75)
  local copies, waits for them, and re-layouts: 5.91 us -> 0.01 us
  Pallas kernels: 31.4 us -> 29.3 us
  other arithmetic: 1.6 us -> 0 us
    unnamed x12 -> x2, local copies, waits for them, and re-layouts: 4.45 us -> 0.01 us
    pallas_call x1 -> x2, Pallas kernels: 31.4 us -> 29.3 us  [the longest x1 27.3 us: shards(): pl.pallas_call(kernel, out_shape=[jax.ShapeDtypeStruct((ROWS, CELLS), F32...]
    mul x1 -> x0, other arithmetic: 1.6 us -> none  [shards(): return -level_coef[None, :, None] * second]
    reshape x2 -> x0, local copies, waits for them, and re-layouts: 1.46 us -> none  [the longest x1 0.73 us: shards(): dc_edge.reshape(1, -1)]
where the time goes in v2:
time: 29.4 us; the launch traced here: 29.3 us
  Pallas kernels  29.3 us (100%)
    pallas_call x1, Pallas kernels, shards(): pl.pallas_call(kernel, out_shape=[jax.ShapeDtypeStruct((ROWS, CELLS), F32...  27.3 us
    pallas_call x1, Pallas kernels, shards(): pl.pallas_call(finish, out_shape=jax.ShapeDtypeStruct(field.shape, F32),...  2.06 us

profile of v2, /device:TPU:1, one launch (start us, length us, event | category | flops | bytes accessed | tf_op | source)
XLA Modules:
  0.0 29.3 jit_solution(7727960442887796513)
XLA Ops:
  0.0 0.0 copy-start
  0.0 27.3 %diffusion.1 = (f32[512,1024]{1,0:T(8,128)S(1)}, bf16[512,256]{1,0:T(8,128)(2,1)S(1)}, bf16[512,256]{1,0:T(8,128)(2,1)S(1)}, bf16[256,1024]{1,0:T(8,128)(2,1)S(1)}, bf16[256,1024]{1,0:T(8,128)(2,1)S(1)}) custom-call(f32[9,55,1024]{2,1,0:T(8,128)} %field.1, f32[1024]{0:T(1024)} %area_in.1, f32[3232]{0:T(1024)} %dv_in.1, f32[3232]{0:T(1024)} %dc_in.1, ...), custom_call_target="tpu_custom_call" | custom-call | tf_op jit(solution)/shard_map/diffusion/pallas_call | solution.py:384
  27.3 0.0 copy-done
  27.3 2.1 %finish.1 = f32[9,55,1024]{2,1,0:T(8,128)} custom-call(f32[512,1024]{1,0:T(8,128)S(1)} %get-tuple-element.10.acc, bf16[512,256]{1,0:T(8,128)(2,1)S(1)} %get-tuple-element.11.halo_h, bf16[512,256]{1,0:T(8,128)(2,1)S(1)} %get-tuple-element.12.halo_l, bf16[256,1024]{1,0:T(8,128)(2,1)S(1)} %get-tuple-element.13.rim_h, ...), custom_call_target="tpu_custom_call" | custom-call | tf_op jit(solution)/shard_map/finish/pallas_call | solution.py:437
Async XLA Ops:
  0.0 27.3 %copy-start = (f32[55]{0:T(128)S(1)}, f32[55]{0:T(128)}, u32[]{:S(2)}) copy-start(f32[55]{0:T(128)} %param.15) | copy-start | bytes 664

commit v3 on v2

--- a/solution.py
+++ b/solution.py
@@ -11,6 +11,7 @@
 F32 = jnp.float32
 BF16 = jnp.bfloat16
 I32 = jnp.int32
+I16 = jnp.int16
 
 BLOCK_ROW = 16
 SIDE = 16
@@ -72,7 +73,8 @@
     lh,
     ll,
     near,
-    coef,
+    coef_h,
+    coef_l,
     diag,
     send_up,
     send_down,
@@ -208,10 +210,12 @@
         corner_b = got_corner[k, h, 1]
         shape = (part, 128)
         lane = lanes(shape)
-        own = (lane & 31) == rows_of(shape)
+        per_row = 32 // part
         corners = jnp.where(lanes((corner_rows, 128)) < 96, corner_a, corner_b)
         for g in range(8):
-            spread = jnp.where(own, jnp.broadcast_to(corners[g : g + 1], shape), 0.0)
+            row = g // per_row
+            own = (lane & 31) == rows_of(shape) + part * (g % per_row)
+            spread = jnp.where(own, jnp.broadcast_to(corners[row : row + 1], shape), 0.0)
             from_left = right if g == 0 else pltpu.roll(right, 128 - 16 * g, 1)
             from_right = left if g == 1 else pltpu.roll(left, (144 - 16 * g) % 128, 1)
             piece = jnp.where(
@@ -288,36 +292,39 @@
         other = jnp.where(other < CELLS, other, start + place)
         near[:, cols] = jnp.where(valid, other, -1)
         factor = jnp.where(valid, ratio / area[cols].reshape(1, 128), 0.0)
-        high, low = split(factor)
-        factor = high.astype(F32) + low.astype(F32)
-        coef[:, cols] = factor
-        diag[0:1, cols] = jnp.sum(factor, axis=0, keepdims=True)
-
+        high, low = (piece.astype(F32) for piece in split(factor))
+        coef_h[:, cols] = high
+        coef_l[:, cols] = low
+        diag[0:1, cols] = jnp.sum(high + low, axis=0, keepdims=True)
+
+    block = (16, 128)
     for t in range(CELLS // 128):
         cols = slice(128 * t, 128 * t + 128)
-        nears = [jnp.broadcast_to(near[j : j + 1, cols], (16, 128)) for j in range(6)]
-        coefs = [jnp.broadcast_to(coef[j : j + 1, cols], (16, 128)) for j in range(6)]
-
-        def put(high_ref, low_ref, at_row, ids, cols=cols, nears=nears, coefs=coefs):
-            value = jnp.where(ids == nears[0], coefs[0], 0.0)
-            for j in range(1, 6):
-                value = jnp.where(ids == nears[j], coefs[j], value)
-            high, low = split(value)
+        nears = [jnp.broadcast_to(near[j : j + 1, cols], block).astype(I16) for j in range(6)]
+        highs = [jnp.broadcast_to(coef_h[j : j + 1, cols], block).astype(BF16) for j in range(6)]
+        lows = [jnp.broadcast_to(coef_l[j : j + 1, cols], block).astype(BF16) for j in range(6)]
+
+        def put(high_ref, low_ref, at_row, ids, cols=cols, nears=nears, highs=highs, lows=lows):
+            high = jnp.zeros(block, BF16)
+            low = jnp.zeros(block, BF16)
+            for j in range(6):
+                here = ids == nears[j]
+                high = jnp.where(here, highs[j], high)
+                low = jnp.where(here, lows[j], low)
             high_ref[pl.ds(at_row, 16), cols] = high
             low_ref[pl.ds(at_row, 16), cols] = low
 
-        def fill(i, carry, put=put):
-            at_row = pl.multiple_of(i * 16, 16)
-            put(lh, ll, at_row, rows_of((16, 128)) + at_row)
-            return carry
-
-        lax.fori_loop(0, CELLS // 16, fill, 0, unroll=8)
+        def fill(i, ids, put=put):
+            put(lh, ll, pl.multiple_of(i * 16, 16), ids)
+            return ids + jnp.full(block, 16, I16)
+
+        ids = lax.fori_loop(0, CELLS // 16, fill, rows_of(block).astype(I16), unroll=8)
         for at_row in range(0, HALO, 16):
-            ids = rows_of((16, 128)) + (CELLS + at_row)
             if CELLS + at_row >= CORNER_A:
                 corner = CORNER_A if CELLS + at_row < CORNER_B else CORNER_B
-                ids = jnp.full((16, 128), corner, I32)
+                ids = jnp.full(block, corner, I16)
             put(rim_h, rim_l, at_row, ids)
+            ids = ids + jnp.full(block, 16, I16)
 
     tiles = [slice(256 * n, 256 * n + 256) for n in range(CELLS // 256)]
 
@@ -328,10 +335,7 @@
             a += dot(xl[...], lh[:, cols])
             acc[:, cols] = a - diag[0:1, cols] * acc[:, cols]
 
-    own_part()
-    copies_b = []
-    for h in range(CHUNKS):
-        receive(0, h, copies_a[h])
+    def halo_part(h, then=None):
         here = pl.ds(h * CHUNK, CHUNK)
         for cols in tiles:
             a = dot(halo_h[here, :], rim_h[:, cols])
@@ -339,13 +343,25 @@
             a += dot(halo_l[here, :], rim_h[:, cols])
             value = acc[here, cols] + a
             acc[here, cols] = value
-            high, low = split(value)
-            xh[here, cols] = high
-            xl[here, cols] = low
+            if then is not None:
+                then(here, cols, value)
+
+    def keep(here, cols, value):
+        high, low = split(value)
+        xh[here, cols] = high
+        xl[here, cols] = low
+
+    own_part()
+    copies_b = []
+    for h in range(CHUNKS):
+        receive(0, h, copies_a[h])
+        halo_part(h, keep)
         copies_b.append(exchange(1, h))
     own_part()
     for h in range(CHUNKS):
         receive(1, h, copies_b[h])
+        if h < CHUNKS - 1:
+            halo_part(h)
     for h in range(CHUNKS):
         for copy in copies_a[h] + copies_b[h]:
             copy.wait_send()
@@ -355,19 +371,37 @@
     spread = jnp.broadcast_to(level[...], (LEVELS, LEVELS))
     on_diagonal = lanes((LEVELS, LEVELS)) == rows_of((LEVELS, LEVELS))
     scale = -jnp.sum(jnp.where(on_diagonal, spread, 0.0), axis=1, keepdims=True)
+    last = (CHUNKS - 1) * CHUNK
     copies = []
+
+    def put(f):
+        copies.append(pltpu.make_async_copy(result.at[f], out.at[f], sem.at[f]))
+        copies[-1].start()
+
+    for f in range(FIELDS):
+        start = f * PITCH
+        ready = min(LEVELS, max(0, last - start))
+        if ready:
+            result[f, 0:ready, :] = acc[start : start + ready, :] * scale[0:ready]
+        if ready == LEVELS:
+            put(f)
+    tail = pl.ds(last, CHUNK)
     for n in range(CELLS // 256):
         cols = slice(256 * n, 256 * n + 256)
-        a = dot(halo_h[...], rim_h[:, cols])
-        a += dot(halo_h[...], rim_l[:, cols])
-        a += dot(halo_l[...], rim_h[:, cols])
-        value = acc[:, cols] + a
+        a = dot(halo_h[tail, :], rim_h[:, cols])
+        a += dot(halo_h[tail, :], rim_l[:, cols])
+        a += dot(halo_l[tail, :], rim_h[:, cols])
+        value = acc[tail, cols] + a
         for f in range(FIELDS):
-            result[f, :, cols] = value[f * PITCH : f * PITCH + LEVELS] * scale
-        copies.append(
-            pltpu.make_async_copy(result.at[:, :, cols], out.at[:, :, cols], sem.at[n])
-        )
-        copies[-1].start()
+            start = f * PITCH
+            ready = min(LEVELS, max(0, last - start))
+            if ready < LEVELS:
+                result[f, ready:LEVELS, cols] = (
+                    value[start + ready - last : start + LEVELS - last] * scale[ready:LEVELS]
+                )
+    for f in range(FIELDS):
+        if last - f * PITCH < LEVELS:
+            put(f)
     for copy in copies:
         copy.wait()
 
@@ -407,6 +441,7 @@
             pltpu.VMEM((CELLS, CELLS), BF16),
             pltpu.VMEM((8, CELLS), I32),
             pltpu.VMEM((8, CELLS), F32),
+            pltpu.VMEM((8, CELLS), F32),
             pltpu.VMEM((1, CELLS), F32),
             pltpu.VMEM((*ends, half, 128), F32),
             pltpu.VMEM((*ends, half, 128), F32),
@@ -441,7 +476,7 @@
         out_specs=hbm,
         scratch_shapes=[
             pltpu.VMEM((FIELDS, LEVELS, CELLS), F32),
-            pltpu.SemaphoreType.DMA((CELLS // 256,)),
+            pltpu.SemaphoreType.DMA((FIELDS,)),
         ],
         compiler_params=pltpu.CompilerParams(vmem_limit_bytes=40 * 1024 * 1024),
         name="finish",

time: 29.4 us -> 28.8 us (0.980)
  Pallas kernels: 29.3 us -> 28.7 us
    pallas_call x1, Pallas kernels: 2.06 us -> 1.67 us  [shards(): pl.pallas_call(finish, out_shape=jax.ShapeDtypeStruct(field.shape, F32),...]
where the time goes in v3:
time: 28.8 us; the launch traced here: 28.7 us
  Pallas kernels  28.7 us (100%)
    pallas_call x1, Pallas kernels, shards(): pl.pallas_call(kernel, out_shape=[jax.ShapeDtypeStruct((ROWS, CELLS), F32...  27 us
    pallas_call x1, Pallas kernels, shards(): pl.pallas_call(finish, out_shape=jax.ShapeDtypeStruct(field.shape, F32),...  1.67 us

profile of v3, /device:TPU:1, one launch (start us, length us, event | category | flops | bytes accessed | tf_op | source)
XLA Modules:
  0.0 28.7 jit_solution(14993544456870999774)
XLA Ops:
  0.0 0.0 copy-start
  0.0 27.0 %diffusion.1 = (f32[512,1024]{1,0:T(8,128)S(1)}, bf16[512,256]{1,0:T(8,128)(2,1)S(1)}, bf16[512,256]{1,0:T(8,128)(2,1)S(1)}, bf16[256,1024]{1,0:T(8,128)(2,1)S(1)}, bf16[256,1024]{1,0:T(8,128)(2,1)S(1)}) custom-call(f32[9,55,1024]{2,1,0:T(8,128)} %field.1, f32[1024]{0:T(1024)} %area_in.1, f32[3232]{0:T(1024)} %dv_in.1, f32[3232]{0:T(1024)} %dc_in.1, ...), custom_call_target="tpu_custom_call" | custom-call | tf_op jit(solution)/shard_map/diffusion/pallas_call | solution.py:418
  27.0 0.0 copy-done
  27.0 1.7 %finish.1 = f32[9,55,1024]{2,1,0:T(8,128)} custom-call(f32[512,1024]{1,0:T(8,128)S(1)} %get-tuple-element.10.acc, bf16[512,256]{1,0:T(8,128)(2,1)S(1)} %get-tuple-element.11.halo_h, bf16[512,256]{1,0:T(8,128)(2,1)S(1)} %get-tuple-element.12.halo_l, bf16[256,1024]{1,0:T(8,128)(2,1)S(1)} %get-tuple-element.13.rim_h, ...), custom_call_target="tpu_custom_call" | custom-call | tf_op jit(solution)/shard_map/finish/pallas_call | solution.py:472
Async XLA Ops:
  0.0 27.0 %copy-start = (f32[55]{0:T(128)S(1)}, f32[55]{0:T(128)}, u32[]{:S(2)}) copy-start(f32[55]{0:T(128)} %param.15) | copy-start | bytes 664

commit v4 on v3

--- a/solution.py
+++ b/solution.py
@@ -145,40 +145,9 @@
     def exchange(k, h):
         here = pl.ds(h * CHUNK, CHUNK)
         picked = dot(xh[here, :], select[...]) + dot(xl[here, :], select[...])
-        lane = lanes((half, 128))
-        top = picked[:half, :128]
-        low_half = picked[half:, :128]
-        send_up[k, h] = jnp.where(lane < 64, top, pltpu.roll(low_half, 64, 1))
-        send_down[k, h] = jnp.where(lane < 64, pltpu.roll(top, 64, 1), low_half)
-        rest = picked[:, 128:]
-        group = lanes((part, 128)) // 16
-        right = rest[0:part]
-        left = pltpu.roll(rest[0:part], 112, 1)
-        for g in range(1, 8):
-            piece = rest[part * g : part * g + part]
-            right = jnp.where(group == g, pltpu.roll(piece, 16 * g, 1), right)
-            left = jnp.where(group == g, piece if g == 1 else pltpu.roll(piece, 16 * g - 16, 1), left)
-        send_right[k, h] = right
-        send_left[k, h] = left
-        lane32 = lanes((32, 128))
-        own = (lane32 >= 64) & ((lane32 & 31) == rows_of((32, 128)))
-        folded = [
-            jnp.sum(jnp.where(own, rest[32 * g : 32 * g + 32], 0.0), axis=0, keepdims=True)
-            for g in range(corner_rows)
-        ]
-        send_corner[k, h] = jnp.concatenate(folded, axis=0)
-        if k == 0 and h == 0:
-            pl.semaphore_wait(barrier, 6)
-        plan = (
-            (send_up, got_up.at[k, h], offsets[2]),
-            (send_down, got_down.at[k, h], offsets[3]),
-            (send_right, got_right.at[k, h], offsets[0]),
-            (send_left, got_left.at[k, h], offsets[1]),
-            (send_corner, got_corner.at[k, h, 0], offsets[4]),
-            (send_corner, got_corner.at[k, h, 1], offsets[5]),
-        )
         copies = []
-        for i, (src, dst, offset) in enumerate(plan):
+
+        def start(i, src, dst, offset):
             copies.append(
                 pltpu.make_async_remote_copy(
                     src_ref=src.at[k, h],
@@ -190,6 +159,37 @@
                 )
             )
             copies[-1].start()
+
+        rest = picked[:, 128:]
+        lane32 = lanes((32, 128))
+        own = (lane32 >= 64) & ((lane32 & 31) == rows_of((32, 128)))
+        folded = [
+            jnp.sum(jnp.where(own, rest[32 * g : 32 * g + 32], 0.0), axis=0, keepdims=True)
+            for g in range(corner_rows)
+        ]
+        send_corner[k, h] = jnp.concatenate(folded, axis=0)
+        lane = lanes((half, 128))
+        top = picked[:half, :128]
+        low_half = picked[half:, :128]
+        send_up[k, h] = jnp.where(lane < 64, top, pltpu.roll(low_half, 64, 1))
+        send_down[k, h] = jnp.where(lane < 64, pltpu.roll(top, 64, 1), low_half)
+        if k == 0 and h == 0:
+            pl.semaphore_wait(barrier, 6)
+        start(4, send_corner, got_corner.at[k, h, 0], offsets[4])
+        start(5, send_corner, got_corner.at[k, h, 1], offsets[5])
+        start(2, send_up, got_up.at[k, h], offsets[2])
+        start(3, send_down, got_down.at[k, h], offsets[3])
+        group = lanes((part, 128)) // 16
+        right = rest[0:part]
+        left = pltpu.roll(rest[0:part], 112, 1)
+        for g in range(1, 8):
+            piece = rest[part * g : part * g + part]
+            right = jnp.where(group == g, pltpu.roll(piece, 16 * g, 1), right)
+            left = jnp.where(group == g, piece if g == 1 else pltpu.roll(piece, 16 * g - 16, 1), left)
+        send_right[k, h] = right
+        send_left[k, h] = left
+        start(0, send_right, got_right.at[k, h], offsets[0])
+        start(1, send_left, got_left.at[k, h], offsets[1])
         return copies
 
     def receive(k, h, copies):

time: 28.8 us -> 27.3 us (0.948)
  Pallas kernels: 28.7 us -> 27.2 us
    pallas_call x1, Pallas kernels: 27 us -> 25.5 us  [shards(): pl.pallas_call(kernel, out_shape=[jax.ShapeDtypeStruct((ROWS, CELLS), F32...]
where the time goes in v4:
time: 27.3 us; the launch traced here: 27.2 us
  Pallas kernels  27.2 us (100%)
    pallas_call x1, Pallas kernels, shards(): pl.pallas_call(kernel, out_shape=[jax.ShapeDtypeStruct((ROWS, CELLS), F32...  25.5 us
    pallas_call x1, Pallas kernels, shards(): pl.pallas_call(finish, out_shape=jax.ShapeDtypeStruct(field.shape, F32),...  1.67 us

profile of v4, /device:TPU:1, one launch (start us, length us, event | category | flops | bytes accessed | tf_op | source)
XLA Modules:
  0.0 27.2 jit_solution(16222729383954113079)
XLA Ops:
  0.0 0.0 copy-start
  0.0 25.5 %diffusion.1 = (f32[512,1024]{1,0:T(8,128)S(1)}, bf16[512,256]{1,0:T(8,128)(2,1)S(1)}, bf16[512,256]{1,0:T(8,128)(2,1)S(1)}, bf16[256,1024]{1,0:T(8,128)(2,1)S(1)}, bf16[256,1024]{1,0:T(8,128)(2,1)S(1)}) custom-call(f32[9,55,1024]{2,1,0:T(8,128)} %field.1, f32[1024]{0:T(1024)} %area_in.1, f32[3232]{0:T(1024)} %dv_in.1, f32[3232]{0:T(1024)} %dc_in.1, ...), custom_call_target="tpu_custom_call" | custom-call | tf_op jit(solution)/shard_map/diffusion/pallas_call | solution.py:418
  25.6 0.0 copy-done
  25.6 1.7 %finish.1 = f32[9,55,1024]{2,1,0:T(8,128)} custom-call(f32[512,1024]{1,0:T(8,128)S(1)} %get-tuple-element.10.acc, bf16[512,256]{1,0:T(8,128)(2,1)S(1)} %get-tuple-element.11.halo_h, bf16[512,256]{1,0:T(8,128)(2,1)S(1)} %get-tuple-element.12.halo_l, bf16[256,1024]{1,0:T(8,128)(2,1)S(1)} %get-tuple-element.13.rim_h, ...), custom_call_target="tpu_custom_call" | custom-call | tf_op jit(solution)/shard_map/finish/pallas_call | solution.py:472
Async XLA Ops:
  0.0 25.6 %copy-start = (f32[55]{0:T(128)S(1)}, f32[55]{0:T(128)}, u32[]{:S(2)}) copy-start(f32[55]{0:T(128)} %param.15) | copy-start | bytes 664

commit v5 on v4

--- a/solution.py
+++ b/solution.py
@@ -107,13 +107,14 @@
         return copy
 
     list_load = load(FIELDS, send_in, send)
-    loads = [load(f, field.at[f], xf.at[f]) for f in range(FIELDS)]
     table_loads = [
         load(FIELDS + 1 + i, src, dst)
         for i, (src, dst) in enumerate(
             ((beside_in, beside), (ends_in, ends), (dv_in, dv), (dc_in, dc), (area_in, area))
         )
     ]
+
+    loads = [load(f, field.at[f], xf.at[f]) for f in range(FIELDS)]
 
     list_load.wait()
     lists = send[...]
@@ -226,21 +227,6 @@
             high, low = split(piece)
             halo_h[pl.ds(h * CHUNK + part * g, part), 128:256] = high
             halo_l[pl.ds(h * CHUNK + part * g, part), 128:256] = low
-
-    pad = jnp.zeros((PITCH - LEVELS, CELLS), F32)
-    acc[FIELDS * PITCH : ROWS, :] = jnp.zeros((ROWS - FIELDS * PITCH, CELLS), F32)
-    copies_a = []
-    waited = 0
-    for h in range(CHUNKS):
-        while waited < FIELDS and waited * PITCH < (h + 1) * CHUNK:
-            loads[waited].wait()
-            acc[pl.ds(waited * PITCH, PITCH), :] = jnp.concatenate([xf[waited], pad], axis=0)
-            waited += 1
-        here = pl.ds(h * CHUNK, CHUNK)
-        high, low = split(acc[here, :])
-        xh[here, :] = high
-        xl[here, :] = low
-        copies_a.append(exchange(0, h))
 
     for copy in table_loads:
         copy.wait()
@@ -297,39 +283,56 @@
         coef_l[:, cols] = low
         diag[0:1, cols] = jnp.sum(high + low, axis=0, keepdims=True)
 
+    pad = jnp.zeros((PITCH - LEVELS, CELLS), F32)
+    acc[FIELDS * PITCH : ROWS, :] = jnp.zeros((ROWS - FIELDS * PITCH, CELLS), F32)
+    copies_a = []
+    waited = 0
+    for h in range(CHUNKS):
+        while waited < FIELDS and waited * PITCH < (h + 1) * CHUNK:
+            loads[waited].wait()
+            acc[pl.ds(waited * PITCH, PITCH), :] = jnp.concatenate([xf[waited], pad], axis=0)
+            waited += 1
+        here = pl.ds(h * CHUNK, CHUNK)
+        high, low = split(acc[here, :])
+        xh[here, :] = high
+        xl[here, :] = low
+        copies_a.append(exchange(0, h))
+
     block = (16, 128)
-    for t in range(CELLS // 128):
+    first_ids = rows_of(block).astype(I16)
+
+    def build(t):
         cols = slice(128 * t, 128 * t + 128)
         nears = [jnp.broadcast_to(near[j : j + 1, cols], block).astype(I16) for j in range(6)]
         highs = [jnp.broadcast_to(coef_h[j : j + 1, cols], block).astype(BF16) for j in range(6)]
         lows = [jnp.broadcast_to(coef_l[j : j + 1, cols], block).astype(BF16) for j in range(6)]
 
-        def put(high_ref, low_ref, at_row, ids, cols=cols, nears=nears, highs=highs, lows=lows):
+        def put(high_ref, low_ref, at_row, ids):
             high = jnp.zeros(block, BF16)
             low = jnp.zeros(block, BF16)
             for j in range(6):
                 here = ids == nears[j]
                 high = jnp.where(here, highs[j], high)
                 low = jnp.where(here, lows[j], low)
-            high_ref[pl.ds(at_row, 16), cols] = high
-            low_ref[pl.ds(at_row, 16), cols] = low
-
-        def fill(i, ids, put=put):
-            put(lh, ll, pl.multiple_of(i * 16, 16), ids)
-            return ids + jnp.full(block, 16, I16)
-
-        ids = lax.fori_loop(0, CELLS // 16, fill, rows_of(block).astype(I16), unroll=8)
+            high_ref[at_row : at_row + 16, cols] = high
+            low_ref[at_row : at_row + 16, cols] = low
+
+        for at_row in range(0, CELLS, 16):
+            put(lh, ll, at_row, first_ids + jnp.full(block, at_row, I16))
         for at_row in range(0, HALO, 16):
+            ids = first_ids + jnp.full(block, CELLS + at_row, I16)
             if CELLS + at_row >= CORNER_A:
                 corner = CORNER_A if CELLS + at_row < CORNER_B else CORNER_B
                 ids = jnp.full(block, corner, I16)
             put(rim_h, rim_l, at_row, ids)
-            ids = ids + jnp.full(block, 16, I16)
 
     tiles = [slice(256 * n, 256 * n + 256) for n in range(CELLS // 256)]
 
-    def own_part():
-        for cols in tiles:
+    def own_part(building=False):
+        for n, cols in enumerate(tiles):
+            if building and n + 1 < len(tiles):
+                build(2 * n + 2)
+                build(2 * n + 3)
             a = dot(xh[...], lh[:, cols])
             a += dot(xh[...], ll[:, cols])
             a += dot(xl[...], lh[:, cols])
@@ -351,7 +354,9 @@
         xh[here, cols] = high
         xl[here, cols] = low
 
-    own_part()
+    build(0)
+    build(1)
+    own_part(building=True)
     copies_b = []
     for h in range(CHUNKS):
         receive(0, h, copies_a[h])

time: 27.3 us -> 27.1 us (level)
  no operation moved by 1% of the time
where the time goes in v5:
time: 27.1 us; the launch traced here: 27 us
  Pallas kernels  27 us (100%)
    pallas_call x1, Pallas kernels, shards(): pl.pallas_call(kernel, out_shape=[jax.ShapeDtypeStruct((ROWS, CELLS), F32...  25.3 us
    pallas_call x1, Pallas kernels, shards(): pl.pallas_call(finish, out_shape=jax.ShapeDtypeStruct(field.shape, F32),...  1.67 us

profile of v5, /device:TPU:1, one launch (start us, length us, event | category | flops | bytes accessed | tf_op | source)
XLA Modules:
  0.0 27.0 jit_solution(5156863364387460637)
XLA Ops:
  0.0 0.0 copy-start
  0.0 25.3 %diffusion.1 = (f32[512,1024]{1,0:T(8,128)S(1)}, bf16[512,256]{1,0:T(8,128)(2,1)S(1)}, bf16[512,256]{1,0:T(8,128)(2,1)S(1)}, bf16[256,1024]{1,0:T(8,128)(2,1)S(1)}, bf16[256,1024]{1,0:T(8,128)(2,1)S(1)}) custom-call(f32[9,55,1024]{2,1,0:T(8,128)} %field.1, f32[1024]{0:T(1024)} %area_in.1, f32[3232]{0:T(1024)} %dv_in.1, f32[3232]{0:T(1024)} %dc_in.1, ...), custom_call_target="tpu_custom_call" | custom-call | tf_op jit(solution)/shard_map/diffusion/pallas_call | solution.py:423
  25.3 0.0 copy-done
  25.3 1.7 %finish.1 = f32[9,55,1024]{2,1,0:T(8,128)} custom-call(f32[512,1024]{1,0:T(8,128)S(1)} %get-tuple-element.10.acc, bf16[512,256]{1,0:T(8,128)(2,1)S(1)} %get-tuple-element.11.halo_h, bf16[512,256]{1,0:T(8,128)(2,1)S(1)} %get-tuple-element.12.halo_l, bf16[256,1024]{1,0:T(8,128)(2,1)S(1)} %get-tuple-element.13.rim_h, ...), custom_call_target="tpu_custom_call" | custom-call | tf_op jit(solution)/shard_map/finish/pallas_call | solution.py:477
Async XLA Ops:
  0.0 25.3 %copy-start = (f32[55]{0:T(128)S(1)}, f32[55]{0:T(128)}, u32[]{:S(2)}) copy-start(f32[55]{0:T(128)} %param.15) | copy-start | bytes 664

commit v6 on v5

--- a/solution.py
+++ b/solution.py
@@ -390,6 +390,7 @@
             result[f, 0:ready, :] = acc[start : start + ready, :] * scale[0:ready]
         if ready == LEVELS:
             put(f)
+    early = len(copies)
     tail = pl.ds(last, CHUNK)
     for n in range(CELLS // 256):
         cols = slice(256 * n, 256 * n + 256)
@@ -404,9 +405,13 @@
                 result[f, ready:LEVELS, cols] = (
                     value[start + ready - last : start + LEVELS - last] * scale[ready:LEVELS]
                 )
-    for f in range(FIELDS):
-        if last - f * PITCH < LEVELS:
-            put(f)
+        rest = pl.ds(early, FIELDS - early)
+        copies.append(
+            pltpu.make_async_copy(
+                result.at[rest, :, cols], out.at[rest, :, cols], sem.at[early + n]
+            )
+        )
+        copies[-1].start()
     for copy in copies:
         copy.wait()
 

time: 27.1 us -> 27 us (level)
  no operation moved by 1% of the time
where the time goes in v6:
time: 27 us
  Pallas kernels  26.9 us (100%)
    pallas_call x1, Pallas kernels, shards(): pl.pallas_call(kernel, out_shape=[jax.ShapeDtypeStruct((ROWS, CELLS), F32...  25.3 us
    pallas_call x1, Pallas kernels, shards(): pl.pallas_call(finish, out_shape=jax.ShapeDtypeStruct(field.shape, F32),...  1.62 us

profile of v6, /device:TPU:1, one launch (start us, length us, event | category | flops | bytes accessed | tf_op | source)
XLA Modules:
  0.0 27.0 jit_solution(15719418752698993334)
XLA Ops:
  0.0 0.0 copy-start
  0.0 25.3 %diffusion.1 = (f32[512,1024]{1,0:T(8,128)S(1)}, bf16[512,256]{1,0:T(8,128)(2,1)S(1)}, bf16[512,256]{1,0:T(8,128)(2,1)S(1)}, bf16[256,1024]{1,0:T(8,128)(2,1)S(1)}, bf16[256,1024]{1,0:T(8,128)(2,1)S(1)}) custom-call(f32[9,55,1024]{2,1,0:T(8,128)} %field.1, f32[1024]{0:T(1024)} %area_in.1, f32[3232]{0:T(1024)} %dv_in.1, f32[3232]{0:T(1024)} %dc_in.1, ...), custom_call_target="tpu_custom_call" | custom-call | tf_op jit(solution)/shard_map/diffusion/pallas_call | solution.py:428
  25.3 0.0 copy-done
  25.3 1.6 %finish.1 = f32[9,55,1024]{2,1,0:T(8,128)} custom-call(f32[512,1024]{1,0:T(8,128)S(1)} %get-tuple-element.10.acc, bf16[512,256]{1,0:T(8,128)(2,1)S(1)} %get-tuple-element.11.halo_h, bf16[512,256]{1,0:T(8,128)(2,1)S(1)} %get-tuple-element.12.halo_l, bf16[256,1024]{1,0:T(8,128)(2,1)S(1)} %get-tuple-element.13.rim_h, ...), custom_call_target="tpu_custom_call" | custom-call | tf_op jit(solution)/shard_map/finish/pallas_call | solution.py:482
Async XLA Ops:
  0.0 25.3 %copy-start = (f32[55]{0:T(128)S(1)}, f32[55]{0:T(128)}, u32[]{:S(2)}) copy-start(f32[55]{0:T(128)} %param.15) | copy-start | bytes 664
